TPU v7x, 32 devices: a whole 2x2x4 slice. The times are simulated.
32 devices in a mesh: grp: 2 (over y), tx: 4 (over z), ty: 4 (over x, core).
Axes of the slice: x: 2, y: 2, z: 4, core: 2. Of those that a mesh axis runs over, the one named last changes fastest.
Arguments:
- obj_field: float32 [2, 1024, 512], P(None, ('grp', 'tx'), 'ty'), parts along dimension 1, may hold values from -6 to 6
- eigenprobes: bfloat16 [2, 32, 128, 128], P(None, 'grp'), parts along dimension 1, may hold values from -1.5 to 1.5
- weights: float32 [8, 4, 3, 16], P(('grp', 'tx'), 'ty'), parts along dimension 0, may hold values from -4 to 4
- offsets: int32 [8, 4, 3, 2], P(('grp', 'tx'), 'ty'), parts along dimension 0, may hold values from 0 to 127
- counts: int32 [8, 4], P(('grp', 'tx'), 'ty'), parts along dimension 0, may hold values from 1 to 3, as said below
- amplitudes: bfloat16 [8, 4, 3, 128, 128], P(('grp', 'tx'), 'ty'), parts along dimension 0, may hold values from 0.19921875 to 3
Outputs:
- new_object: float32 [2, 1024, 512], P(None, ('grp', 'tx'), 'ty'), parts along dimension 1
- new_eigenprobes: float32 [2, 32, 128, 128], P(None, 'grp'), parts along dimension 1
There are 2 independent parts, one for each index of `grp`. A program takes and returns all parts, laid end to end along the dimension named above; each array names one. Nothing has to cross between parts.
Inputs may be any that keep to these rules, and one draw needn't show every extreme that they name: Every tile holds 1 to 3 positions; some tile holds exactly 3; slots from counts on are unused.
All inputs are finite; a program needn't handle non-finite values.
Results may differ from a plain program's by a relative error of at most 0.0003.
Values sent between devices are 32-bit elements; how exact they have to be, the bound alone decides.
A program may use at most 64 MiB of HBM per device.

v0:
```python
import math
import jax
import jax.numpy as jnp
from jax import lax
from jax.sharding import PartitionSpec as P

high = lax.Precision.HIGHEST


def from_behind(value, axis, steps):
    count = lax.axis_size(axis)
    pairs = [(source, (source + steps) % count) for source in range(count)]
    return lax.ppermute(value, axis, pairs)


def tables(frame, sign):
    grid = jnp.arange(frame, dtype=jnp.int32)
    phase = grid[:, None] * grid[None, :] % frame
    angle = phase.astype(jnp.float32) * (2.0 * math.pi / frame)
    scale = 1.0 / math.sqrt(frame)
    return (jnp.cos(angle) * scale, sign * jnp.sin(angle) * scale)


def transform(real_part, imag_part, table_re, table_im):
    left_re = jnp.einsum("jk,skl->sjl", table_re, real_part, precision=high) - jnp.einsum(
        "jk,skl->sjl", table_im, imag_part, precision=high
    )
    left_im = jnp.einsum("jk,skl->sjl", table_re, imag_part, precision=high) + jnp.einsum(
        "jk,skl->sjl", table_im, real_part, precision=high
    )
    out_re = jnp.einsum("sjk,kl->sjl", left_re, table_re, precision=high) - jnp.einsum(
        "sjk,kl->sjl", left_im, table_im, precision=high
    )
    out_im = jnp.einsum("sjk,kl->sjl", left_re, table_im, precision=high) + jnp.einsum(
        "sjk,kl->sjl", left_im, table_re, precision=high
    )
    return (out_re, out_im)


def row_divisor(norms, start, count, frame, modes):
    mode_of_row = (start + jnp.arange(count, dtype=jnp.int32)) // frame % modes
    match = mode_of_row[:, None] == jnp.arange(modes, dtype=jnp.int32)[None, :]
    return jnp.sum(jnp.where(match, norms[None, :] + 1.0, 0.0), axis=1)


def per_device(obj_field, eigenprobes, weights, offsets, counts, amplitudes):
    tile = obj_field.shape[1]
    modes = eigenprobes.shape[1]
    frame = eigenprobes.shape[2]
    slots = weights.shape[2]
    wts = weights[0, 0]
    offs = offsets[0, 0]
    live = (jnp.arange(slots, dtype=jnp.int32) < counts[0, 0]).astype(jnp.float32)
    local_norms = jnp.sum(live[:, None] * wts * wts, axis=0)
    below = from_behind(obj_field, "tx", -1)
    tall = jnp.concatenate([obj_field, below], axis=1)
    beside = from_behind(tall, "ty", -1)
    region = jnp.concatenate([tall, beside], axis=2)
    zero_index = jnp.int32(0)

    def read_window(row_start, col_start):
        return lax.dynamic_slice(region, (zero_index, row_start, col_start), (2, frame, frame))

    windows = jax.vmap(read_window)(offs[:, 0], offs[:, 1])
    win_re = windows[:, 0]
    win_im = windows[:, 1]
    eig32 = eigenprobes.astype(jnp.float32)
    probe = jnp.einsum("sk,ckij->csij", wts, eig32, precision=high)
    psi_re = probe[0] * win_re - probe[1] * win_im
    psi_im = probe[0] * win_im + probe[1] * win_re
    fwd_re, fwd_im = tables(frame, -1.0)
    spec_re, spec_im = transform(psi_re, psi_im, fwd_re, fwd_im)
    amps = amplitudes[0, 0].astype(jnp.float32)
    factor = (amps / jnp.sqrt(spec_re * spec_re + spec_im * spec_im + 0.25) - 1.0) * live[
        :, None, None
    ]
    inv_re, inv_im = tables(frame, 1.0)
    chi_re, chi_im = transform(spec_re * factor, spec_im * factor, inv_re, inv_im)
    obj_re = probe[0] * chi_re + probe[1] * chi_im
    obj_im = probe[0] * chi_im - probe[1] * chi_re
    power = (probe[0] * probe[0] + probe[1] * probe[1]) * live[:, None, None]
    pieces = jnp.stack([obj_re, obj_im, power], axis=1)

    def add_slot(slot, acc):
        row_start = offs[slot, 0]
        col_start = offs[slot, 1]
        piece = lax.dynamic_index_in_dim(pieces, slot, 0, keepdims=False)
        current = lax.dynamic_slice(acc, (zero_index, row_start, col_start), (3, frame, frame))
        return lax.dynamic_update_slice(acc, current + piece, (zero_index, row_start, col_start))

    acc = jnp.zeros((3, tile + frame, tile + frame), jnp.float32)
    acc = lax.fori_loop(0, slots, add_slot, acc)
    grad_re = win_re * chi_re + win_im * chi_im
    grad_im = win_re * chi_im - win_im * chi_re
    slot_grad = jnp.stack([grad_re, grad_im])
    spilled = from_behind(acc[:, :, tile:], "ty", 1)
    merged = acc[:, :, :tile].at[:, :, :frame].add(spilled)
    dropped = from_behind(merged[:, tile:, :], "tx", 1)
    totals = merged[:, :tile, :].at[:, :frame, :].add(dropped)
    local_illum = jnp.sum(totals[2])
    norms, illum_sum = lax.psum((local_norms, local_illum), ("tx", "ty"))
    cells = lax.axis_size("tx") * lax.axis_size("ty") * tile * tile
    mean_illum = illum_sum / cells
    new_object = obj_field + totals[:2] / (totals[2] + mean_illum)[None]
    flat_rows = 2 * modes * frame
    flat_eig = eig32.reshape(flat_rows, frame)
    gprobe = jnp.einsum("sk,csij->ckij", wts, slot_grad, precision=high)
    flat_grad = gprobe.reshape(flat_rows, frame)
    share_rows = flat_rows // (lax.axis_size("tx") * lax.axis_size("ty"))
    start = lax.axis_index(("tx", "ty")) * share_rows
    share = lax.psum_scatter(flat_grad, ("tx", "ty"), scatter_dimension=0, tiled=True)
    own = lax.dynamic_slice_in_dim(flat_eig, start, share_rows, 0)
    updated = own + share / row_divisor(norms, start, share_rows, frame, modes)[:, None]
    new_eig = lax.all_gather(updated, ("tx", "ty"), axis=0, tiled=True).reshape(
        2, modes, frame, frame
    )
    return (new_object, new_eig)


def solution(mesh):
    return jax.shard_map(
        per_device,
        mesh=mesh,
        in_specs=(
            P(None, ("grp", "tx"), "ty"),
            P(None, "grp", None, None),
            P(("grp", "tx"), "ty", None, None),
            P(("grp", "tx"), "ty", None, None),
            P(("grp", "tx"), "ty"),
            P(("grp", "tx"), "ty", None, None, None),
        ),
        out_specs=(P(None, ("grp", "tx"), "ty"), P(None, "grp", None, None)),
        check_vma=False,
    )
```

profile of v0, /device:TPU:0, one launch (start us, length us, event | category | flops | bytes accessed | tf_op | source)
XLA Modules:
  0.0 176.3 jit_solution(10866427820670619271)
XLA Ops:
  7.2 5.1 %collective-permute-start = (f32[2,128,128]{2,1,0:T(8,128)}, f32[2,128,128]{2,1,0:T(8,128)S(1)}, u32[]{:S(2)}, u32[]{:S(2)}) collective-permute-start(f32[2,128,128]{2,1,0:T(8,128)} %param.16), channel_id=1, source_target_pairs={{0,12},{4,0},{8,4},{12,8},{1,13},{5,1},{9,5},{13,9},{2,14},{6,2},{... | collective-permute-start | bytes 393224 | tf_op jit(solution)/shard_map/ppermute | solution.py:13
  13.0 0.8 compare_select_fusion.1
  13.9 0.9 constant_dynamic-update-slice_fusion.1
  14.8 0.6 collective-permute-done
  15.4 0.1 collective-permute-start.1
  15.6 2.2 %convolution_bitcast_fusion.1 = f32[2,3,128,128]{3,1,2,0:T(4,128)S(1)} fusion(bf16[2,16,128,128]{3,2,1,0:T(8,128)(2,1)} %param.17, f32[1,1,3,16]{3,1,2,0:T(1,128)} %param.18), kind=kOutput, calls=%fused_computation.7 | convolution fusion | flops 18874368 | bytes 1441984 | tf_op jit(solution)/shard_map/sk,ckij->csij/dot_general | solution.py:68
  17.8 1.7 collective-permute-done.1
  19.5 15.2 %while.19 = (s32[]{:T(128)}, f32[2,256,256]{2,1,0:T(8,128)S(1)}, s32[3,3]{1,0:T(4,128)S(1)}, f32[3,2,128,128]{3,0,2,1:T(4,128)S(1)}, s32[]{:T(128)}, /*index=5*/s32[]{:T(128)}) while((s32[]{:T(128)}, f32[2,256,256]{2,1,0:T(8,128)S(1)}, s32[3,3]{1,0:T(4,128)S(1)}, f32[3,2,128,128]{3,0,2,1:T(4,128)S(1)}, s32[]{:T(128)}, /*index=5*/s32[]{:T(128)}) %tuple.75), condition=%wide.while_cond.2, body=%wide.while_body.2.sunk | while | flops 2 | bytes 524421 | solution.py:62
  19.5 0.6 fusion.181
  20.1 1.3 constant_dynamic-slice_fusion.12
  21.4 3.1 %dynamic-update-slice.11 = f32[3,2,128,128]{3,0,2,1:T(4,128)S(1)} dynamic-update-slice(f32[3,2,128,128]{3,0,2,1:T(4,128)S(1)} %get-tuple-element.253, f32[1,2,128,128]{3,0,2,1:T(1,128)S(1)} %bitcast.173, s32[]{:T(128)S(6)} %copy.157, s32[]{:T(128)} %constant.159.clone.1..sunk.1, s32[]{:T(128)} %constant.159.clone.1..sunk.1, s32[]{:T(128)} %constant.159.clone.1..sunk.1) | dynamic-update-slice | bytes 262148 | tf_op jit(solution)/shard_map/vmap()/gather
  24.5 0.6 fusion.181
  25.1 1.3 constant_dynamic-slice_fusion.12
  26.4 3.1 %dynamic-update-slice.11 = f32[3,2,128,128]{3,0,2,1:T(4,128)S(1)} dynamic-update-slice(f32[3,2,128,128]{3,0,2,1:T(4,128)S(1)} %get-tuple-element.253, f32[1,2,128,128]{3,0,2,1:T(1,128)S(1)} %bitcast.173, s32[]{:T(128)S(6)} %copy.157, s32[]{:T(128)} %constant.159.clone.1..sunk.1, s32[]{:T(128)} %constant.159.clone.1..sunk.1, s32[]{:T(128)} %constant.159.clone.1..sunk.1) | dynamic-update-slice | bytes 262148 | tf_op jit(solution)/shard_map/vmap()/gather
  29.5 0.6 fusion.181
  30.1 1.3 constant_dynamic-slice_fusion.12
  31.4 3.1 %dynamic-update-slice.11 = f32[3,2,128,128]{3,0,2,1:T(4,128)S(1)} dynamic-update-slice(f32[3,2,128,128]{3,0,2,1:T(4,128)S(1)} %get-tuple-element.253, f32[1,2,128,128]{3,0,2,1:T(1,128)S(1)} %bitcast.173, s32[]{:T(128)S(6)} %copy.157, s32[]{:T(128)} %constant.159.clone.1..sunk.1, s32[]{:T(128)} %constant.159.clone.1..sunk.1, s32[]{:T(128)} %constant.159.clone.1..sunk.1) | dynamic-update-slice | bytes 262148 | tf_op jit(solution)/shard_map/vmap()/gather
  34.7 0.1 fusion.9
  34.8 0.1 copy.63
  34.9 0.6 fusion.50
  35.5 0.1 copy.64
  35.7 0.6 fusion.46
  36.2 0.6 fusion.3
  36.8 0.6 fusion.32
  37.5 0.6 fusion.48
  38.1 0.6 fusion.2
  38.7 0.6 convolution_add_fusion.1
  39.4 0.6 convolution_subtract_fusion.1
  40.0 0.7 fusion.39
  40.8 0.7 fusion.43
  41.5 0.8 fusion
  42.3 0.6 fusion.28
  42.9 0.6 fusion.37
  43.6 0.7 fusion.1
  44.4 0.6 fusion.41
  45.0 0.6 fusion.26
  45.7 0.6 fusion.11
  46.3 2.1 %convolution_bitcast_fusion = f32[2,16,128,128]{3,1,2,0:T(8,128)S(1)} fusion(f32[1,3,128,128]{3,1,2,0:T(4,128)S(1)} %get-tuple-element.177, f32[1,3,128,128]{3,1,2,0:T(4,128)S(1)} %get-tuple-element.176, f32[1,1,3,16]{3,1,2,0:T(1,128)S(1)} %copy-done.3), kind=kOutput, calls=%fused_computation.6 | convolution fusion | flops 18972672 | bytes 2490560 | tf_op jit(solution)/shard_map/sk,csij->ckij/dot_general | solution.py:107
  48.4 1.9 %copy.84 = f32[2,16,128,128]{3,2,1,0:T(8,128)} copy(f32[2,16,128,128]{3,1,2,0:T(8,128)S(1)} %convolution_bitcast_fusion) | data formatting | bytes 4194304 | tf_op jit(solution)/shard_map/sk,csij->ckij/transpose | solution.py:107
  50.6 0.2 pad_maximum_fusion
  50.8 0.3 copy-done.2
  51.1 22.6 %while.18 = (s32[]{:T(128)}, f32[3,256,256]{2,1,0:T(8,128)S(1)}, s32[3,2]{0,1:T(2,128)S(1)}, f32[3,3,128,128]{3,0,2,1:T(4,128)S(1)}, s32[]{:T(128)}, /*index=5*/s32[]{:T(128)}, s32[]{:T(128)}) while((s32[]{:T(128)}, f32[3,256,256]{2,1,0:T(8,128)S(1)}, s32[3,2]{0,1:T(2,128)S(1)}, f32[3,3,128,128]{3,0,2,1:T(4,128)S(1)}, s32[]{:T(128)}, ...), condition=%wide.region_1.2_spmd, body=%wide.region_0.0_spmd.sunk | while | flops 49160 | bytes 1376445 | solution.py:92
  51.1 0.2 constant_dynamic-slice_fusion.9
  51.3 0.7 constant_dynamic-slice_fusion.10
  55.7 0.1 dynamic-slice_add_fusion.2
  55.8 2.8 %dynamic_update_slice.8 = f32[3,256,256]{2,1,0:T(8,128)S(1)} dynamic-update-slice(f32[3,256,256]{2,1,0:T(8,128)S(1)} %get-tuple-element.270, f32[3,128,128]{2,1,0:T(8,128)S(1)} %dynamic-slice_add_fusion.2, s32[]{:T(128)} %constant.159.clone.1..sunk, s32[]{:T(128)S(6)} %select_n.170, s32[]{:T(128)S(6)} %select_n.171) | dynamic-update-slice | bytes 393220 | tf_op jit(solution)/shard_map/while/body/eval_jaxpr/dynamic_update_slice | solution.py:89
  58.6 0.2 constant_dynamic-slice_fusion.9
  58.8 0.7 constant_dynamic-slice_fusion.10
  63.3 0.1 dynamic-slice_add_fusion.2
  63.4 2.7 %dynamic_update_slice.8 = f32[3,256,256]{2,1,0:T(8,128)S(1)} dynamic-update-slice(f32[3,256,256]{2,1,0:T(8,128)S(1)} %get-tuple-element.270, f32[3,128,128]{2,1,0:T(8,128)S(1)} %dynamic-slice_add_fusion.2, s32[]{:T(128)} %constant.159.clone.1..sunk, s32[]{:T(128)S(6)} %select_n.170, s32[]{:T(128)S(6)} %select_n.171) | dynamic-update-slice | bytes 393220 | tf_op jit(solution)/shard_map/while/body/eval_jaxpr/dynamic_update_slice | solution.py:89
  66.1 0.2 constant_dynamic-slice_fusion.9
  66.3 0.7 constant_dynamic-slice_fusion.10
  70.8 0.1 dynamic-slice_add_fusion.2
  70.9 2.8 %dynamic_update_slice.8 = f32[3,256,256]{2,1,0:T(8,128)S(1)} dynamic-update-slice(f32[3,256,256]{2,1,0:T(8,128)S(1)} %get-tuple-element.270, f32[3,128,128]{2,1,0:T(8,128)S(1)} %dynamic-slice_add_fusion.2, s32[]{:T(128)} %constant.159.clone.1..sunk, s32[]{:T(128)S(6)} %select_n.170, s32[]{:T(128)S(6)} %select_n.171) | dynamic-update-slice | bytes 393220 | tf_op jit(solution)/shard_map/while/body/eval_jaxpr/dynamic_update_slice | solution.py:89
  73.7 2.3 %collective-permute-start.2 = (f32[3,256,128]{2,1,0:T(8,128)S(1)}, f32[3,256,128]{2,1,0:T(8,128)S(1)}, u32[]{:S(2)}, u32[]{:S(2)}) collective-permute-start(f32[3,256,128]{2,1,0:T(8,128)S(1)} %slice.92), channel_id=1, source_target_pairs={{0,1},{1,2},{2,3},{3,0},{4,5},{5,6},{6,7},{7,4},{8,9},{9,10},{10,1... | collective-permute-start | bytes 1179656 | tf_op jit(solution)/shard_map/ppermute | solution.py:13
  76.0 5.6 %collective-permute-done.2 = f32[3,256,128]{2,1,0:T(8,128)S(1)} collective-permute-done((f32[3,256,128]{2,1,0:T(8,128)S(1)}, f32[3,256,128]{2,1,0:T(8,128)S(1)}, u32[]{:S(2)}, u32[]{:S(2)}) %collective-permute-start.2) | collective-permute-done | bytes 393248 | tf_op jit(solution)/shard_map/ppermute | solution.py:13
  81.7 0.4 collective-permute-start.3
  82.2 11.8 %collective-permute-done.3 = f32[3,128,128]{2,1,0:T(8,128)S(1)} collective-permute-done((f32[3,128,128]{2,1,0:T(8,128)S(1)}, f32[3,128,128]{2,1,0:T(8,128)S(1)}, u32[]{:S(2)}, u32[]{:S(2)}) %collective-permute-start.3) | collective-permute-done | bytes 196640 | tf_op jit(solution)/shard_map/ppermute | solution.py:13
  94.0 0.6 slice_reduce_fusion
  94.6 30.4 %all-reduce = (f32[]{:T(128)}, f32[16]{0:T(128)S(1)}) all-reduce(f32[]{:T(128)} %slice_reduce_fusion, f32[16]{0:T(128)S(1)} %fusion.80), channel_id=1, replica_groups=mesh['grp'=2,'tx'=4,'ty'=4] {'tx','ty'}, use_global_device_ids=true, to_apply=%region_3.4 | all-reduce | flops 17 | bytes 136 | tf_op jit(solution)/shard_map/psum | solution.py:101
  125.0 1.7 convert_add_fusion
  127.4 0.7 fusion.22
  128.1 38.2 %all-gather.2.cloned.1.call-done = f32[4096,128]{1,0:T(8,128)} async-done(((f32[256,128]{1,0:T(8,128)}), f32[4096,128]{1,0:T(8,128)}) %all-gather.2.cloned.1.call-update) | async-done | bytes 2097168 | tf_op jit(solution)/shard_map/all_gather | solution.py:114
  166.3 3.1 %copy.169 = f32[2,16,128,128]{3,2,1,0:T(8,128)} copy(f32[2,16,128,128]{3,2,1,0:T(8,128)} %bitcast.175) | data formatting | bytes 4194304
  (33 shorter events, 0.8 us)
Async XLA Ops:
  7.2 117.9 %reduce-scatter.2.cloned.1.call-start = ((), (), s32[]{:S(2)}) async-start(), calls=%async_computation.1 | async-start | bytes 2228224 | tf_op jit(solution)/shard_map/reduce_scatter | solution.py:111
  7.2 8.2 %collective-permute-start = (f32[2,128,128]{2,1,0:T(8,128)}, f32[2,128,128]{2,1,0:T(8,128)S(1)}, u32[]{:S(2)}, u32[]{:S(2)}) collective-permute-start(f32[2,128,128]{2,1,0:T(8,128)} %param.16), channel_id=1, source_target_pairs={{0,12},{4,0},{8,4},{12,8},{1,13},{5,1},{9,5},{13,9},{2,14},{6,2},{... | collective-permute-start | bytes 393224 | tf_op jit(solution)/shard_map/ppermute | solution.py:13
  15.4 4.0 %collective-permute-start.1 = (f32[2,256,128]{2,1,0:T(8,128)S(1)}, f32[2,256,128]{2,1,0:T(8,128)S(1)}, u32[]{:S(2)}, u32[]{:S(2)}) collective-permute-start(f32[2,256,128]{2,1,0:T(8,128)S(1)} %constant_dynamic-update-slice_fusion), channel_id=1, source_target_pairs={{0,3},{1,0},{2,1},{3,2},{4,7},{5,4},{6,5},{7,6},{8,11},{9,8},{10,9... | collective-permute-start | bytes 786440 | tf_op jit(solution)/shard_map/ppermute | solution.py:13
  35.5 4.5 %copy-start.1 = (bf16[1,1,3,128,128]{4,3,2,1,0:T(8,128)(2,1)S(1)}, bf16[1,1,3,128,128]{4,3,2,1,0:T(8,128)(2,1)}, u32[]{:S(2)}) copy-start(bf16[1,1,3,128,128]{4,3,2,1,0:T(8,128)(2,1)} %param.21) | copy-start | bytes 294916
  43.6 2.7 %copy-start.3 = (f32[1,1,3,16]{3,1,2,0:T(1,128)S(1)}, f32[1,1,3,16]{3,1,2,0:T(1,128)}, u32[]{:S(2)}) copy-start(f32[1,1,3,16]{3,1,2,0:T(1,128)} %param.18) | copy-start | bytes 580
  50.4 0.7 copy-start.2
  50.4 115.9 %all-gather.2.cloned.1.call-start = ((), (), s32[]{:S(2)}) async-start(), calls=%async_computation.2 | async-start | bytes 2228224 | tf_op jit(solution)/shard_map/all_gather | solution.py:114
  73.7 53.7 %copy-start = (f32[2,128,128]{2,1,0:T(8,128)S(1)}, f32[2,128,128]{2,1,0:T(8,128)}, u32[]{:S(2)}) copy-start(f32[2,128,128]{2,1,0:T(8,128)} %param.16) | copy-start | bytes 393220
  73.7 7.9 %collective-permute-start.2 = (f32[3,256,128]{2,1,0:T(8,128)S(1)}, f32[3,256,128]{2,1,0:T(8,128)S(1)}, u32[]{:S(2)}, u32[]{:S(2)}) collective-permute-start(f32[3,256,128]{2,1,0:T(8,128)S(1)} %slice.92), channel_id=1, source_target_pairs={{0,1},{1,2},{2,3},{3,0},{4,5},{5,6},{6,7},{7,4},{8,9},{9,10},{10,1... | collective-permute-start | bytes 1179656 | tf_op jit(solution)/shard_map/ppermute | solution.py:13
  81.7 12.2 %collective-permute-start.3 = (f32[3,128,128]{2,1,0:T(8,128)S(1)}, f32[3,128,128]{2,1,0:T(8,128)S(1)}, u32[]{:S(2)}, u32[]{:S(2)}) collective-permute-start(f32[3,128,128]{2,1,0:T(8,128)S(1)} %slice.115), channel_id=1, source_target_pairs={{0,4},{4,8},{8,12},{12,0},{1,5},{5,9},{9,13},{13,1},{2,6},{6,10},{... | collective-permute-start | bytes 589832 | tf_op jit(solution)/shard_map/ppermute | solution.py:13
Sparse Core Ops, SparseCore 0:
  50.5 65.2 reduce-scatter.1
  126.8 39.4 all-gather.1
where the time goes:
time: 177 us; the launch traced here: 176 us
  waiting for transfers between devices  57.9 us (33%)
  local copies, waits for them, and re-layouts  32.4 us (18%)
  blocking collectives  30.4 us (17%)
  between operations  15.7 us (9%)
  matrix products  14.7 us (8%)
  loops' own time  11.7 us (7%)
  starting transfers between devices  8.01 us (5%)
  other arithmetic  5.48 us (3%)
    all_gather x1, waiting for transfers between devices, per_device(): lax.all_gather(updated, ('tx', 'ty'), axis=0, tiled=True)  38.2 us
    psum x1, blocking collectives, per_device(): norms, illum_sum = lax.psum((local_norms, local_illum), ('tx', 'ty'))  30.4 us
    ppermute x4, waiting for transfers between devices, from_behind(): return lax.ppermute(value, axis, pairs)  19.7 us
    gather x12, local copies, waits for them, and re-layouts  14.9 us
    another operation x1, loops' own time, per_device(): acc = lax.fori_loop(0, slots, add_slot, acc)  11.4 us
    dynamic_update_slice x3, local copies, waits for them, and re-layouts, add_slot(): lax.dynamic_update_slice(acc, current + piece, (zero_index, row_start, co...  8.27 us
    ppermute x4, starting transfers between devices, from_behind(): return lax.ppermute(value, axis, pairs)  7.93 us
    unnamed x11, local copies, waits for them, and re-layouts  4.42 us
  transfers between devices with their start and end apart: 6, of which 5 were waited for; matrix products, arithmetic and copies ran while one was open for 10% of the time, Pallas kernels for 0%

commit v1 on v0

--- a/solution.py
+++ b/solution.py
@@ -98,7 +98,8 @@
     dropped = from_behind(merged[:, tile:, :], "tx", 1)
     totals = merged[:, :tile, :].at[:, :frame, :].add(dropped)
     local_illum = jnp.sum(totals[2])
-    norms, illum_sum = lax.psum((local_norms, local_illum), ("tx", "ty"))
+    _meet_run = lambda inp: jax.lax.psum(jax.lax.psum(inp, axis_name="ty"), "tx")
+    norms, illum_sum = _meet_run((local_norms, local_illum))
     cells = lax.axis_size("tx") * lax.axis_size("ty") * tile * tile
     mean_illum = illum_sum / cells
     new_object = obj_field + totals[:2] / (totals[2] + mean_illum)[None]

time: 177 us -> 169 us (0.955)
  blocking collectives: 30.4 us -> 16.9 us
  waiting for transfers between devices: 57.9 us -> 64.2 us
    psum x1 -> x2, blocking collectives: 30.4 us -> 16.9 us  [the longest x1 10.7 us: per_device(): jax.lax.psum(jax.lax.psum(inp, axis_name='ty'), 'tx')]
    reduce_scatter x1, waiting for transfers between devices: 0.01 us -> 3.31 us  [per_device(): lax.psum_scatter(flat_grad, ('tx', 'ty'), scatter_dimension=0, tiled=True)]
    all_gather x1, waiting for transfers between devices: 38.2 us -> 40.2 us  [per_device(): lax.all_gather(updated, ('tx', 'ty'), axis=0, tiled=True)]
  transfers between devices with their start and end apart: 6 -> 6, of which waited for: 5 -> 6; matrix products, arithmetic and copies ran while one was open for 10% -> 10% of each run, Pallas kernels for 0% -> 0%
where the time goes in v1:
time: 169 us; the launch traced here: 168 us
  waiting for transfers between devices  64.2 us (38%)
  local copies, waits for them, and re-layouts  32.3 us (19%)
  blocking collectives  16.9 us (10%)
  between operations  15.7 us (9%)
  matrix products  14.7 us (9%)
  loops' own time  11.1 us (7%)
  starting transfers between devices  8 us (5%)
  other arithmetic  5.48 us (3%)
    all_gather x1, waiting for transfers between devices, per_device(): lax.all_gather(updated, ('tx', 'ty'), axis=0, tiled=True)  40.2 us
    ppermute x4, waiting for transfers between devices, from_behind(): return lax.ppermute(value, axis, pairs)  20.7 us
    gather x12, local copies, waits for them, and re-layouts  14.9 us
    another operation x1, loops' own time, per_device(): acc = lax.fori_loop(0, slots, add_slot, acc)  10.8 us
    psum x1, blocking collectives, per_device(): jax.lax.psum(jax.lax.psum(inp, axis_name='ty'), 'tx')  10.7 us
    dynamic_update_slice x3, local copies, waits for them, and re-layouts, add_slot(): lax.dynamic_update_slice(acc, current + piece, (zero_index, row_start, co...  8.27 us
    ppermute x4, starting transfers between devices, from_behind(): return lax.ppermute(value, axis, pairs)  7.92 us
    psum x1, blocking collectives, per_device(): jax.lax.psum(inp, axis_name='ty')  6.27 us
  transfers between devices with their start and end apart: 6, of which 6 were waited for; matrix products, arithmetic and copies ran while one was open for 10% of the time, Pallas kernels for 0%

profile of v1, /device:TPU:0, one launch (start us, length us, event | category | flops | bytes accessed | tf_op | source)
XLA Modules:
  0.0 168.5 jit_solution(2958057151013392547)
XLA Ops:
  7.2 5.1 %collective-permute-start = (f32[2,128,128]{2,1,0:T(8,128)}, f32[2,128,128]{2,1,0:T(8,128)S(1)}, u32[]{:S(2)}, u32[]{:S(2)}) collective-permute-start(f32[2,128,128]{2,1,0:T(8,128)} %param.16), channel_id=1, source_target_pairs={{0,12},{4,0},{8,4},{12,8},{1,13},{5,1},{9,5},{13,9},{2,14},{6,2},{... | collective-permute-start | bytes 393224 | tf_op jit(solution)/shard_map/ppermute | solution.py:13
  13.0 0.8 compare_select_fusion.1
  13.9 0.9 constant_dynamic-update-slice_fusion.1
  14.8 0.6 collective-permute-done
  15.4 0.1 collective-permute-start.1
  15.6 2.2 %convolution_bitcast_fusion.1 = f32[2,3,128,128]{3,1,2,0:T(4,128)S(1)} fusion(bf16[2,16,128,128]{3,2,1,0:T(8,128)(2,1)} %param.17, f32[1,1,3,16]{3,1,2,0:T(1,128)} %param.18), kind=kOutput, calls=%fused_computation.7 | convolution fusion | flops 18874368 | bytes 1441984 | tf_op jit(solution)/shard_map/sk,ckij->csij/dot_general | solution.py:68
  17.8 1.7 collective-permute-done.1
  19.5 15.2 %while.19 = (s32[]{:T(128)}, f32[2,256,256]{2,1,0:T(8,128)S(1)}, s32[3,3]{1,0:T(4,128)S(1)}, f32[3,2,128,128]{3,0,2,1:T(4,128)S(1)}, s32[]{:T(128)}, /*index=5*/s32[]{:T(128)}) while((s32[]{:T(128)}, f32[2,256,256]{2,1,0:T(8,128)S(1)}, s32[3,3]{1,0:T(4,128)S(1)}, f32[3,2,128,128]{3,0,2,1:T(4,128)S(1)}, s32[]{:T(128)}, /*index=5*/s32[]{:T(128)}) %tuple.75), condition=%wide.while_cond.2, body=%wide.while_body.2.sunk | while | flops 2 | bytes 524421 | solution.py:62
  19.5 0.6 fusion.181
  20.1 1.3 constant_dynamic-slice_fusion.12
  21.4 3.1 %dynamic-update-slice.11 = f32[3,2,128,128]{3,0,2,1:T(4,128)S(1)} dynamic-update-slice(f32[3,2,128,128]{3,0,2,1:T(4,128)S(1)} %get-tuple-element.255, f32[1,2,128,128]{3,0,2,1:T(1,128)S(1)} %bitcast.173, s32[]{:T(128)S(6)} %copy.157, s32[]{:T(128)} %constant.159.clone.1..sunk.1, s32[]{:T(128)} %constant.159.clone.1..sunk.1, s32[]{:T(128)} %constant.159.clone.1..sunk.1) | dynamic-update-slice | bytes 262148 | tf_op jit(solution)/shard_map/vmap()/gather
  24.5 0.6 fusion.181
  25.1 1.3 constant_dynamic-slice_fusion.12
  26.4 3.1 %dynamic-update-slice.11 = f32[3,2,128,128]{3,0,2,1:T(4,128)S(1)} dynamic-update-slice(f32[3,2,128,128]{3,0,2,1:T(4,128)S(1)} %get-tuple-element.255, f32[1,2,128,128]{3,0,2,1:T(1,128)S(1)} %bitcast.173, s32[]{:T(128)S(6)} %copy.157, s32[]{:T(128)} %constant.159.clone.1..sunk.1, s32[]{:T(128)} %constant.159.clone.1..sunk.1, s32[]{:T(128)} %constant.159.clone.1..sunk.1) | dynamic-update-slice | bytes 262148 | tf_op jit(solution)/shard_map/vmap()/gather
  29.5 0.6 fusion.181
  30.1 1.3 constant_dynamic-slice_fusion.12
  31.4 3.1 %dynamic-update-slice.11 = f32[3,2,128,128]{3,0,2,1:T(4,128)S(1)} dynamic-update-slice(f32[3,2,128,128]{3,0,2,1:T(4,128)S(1)} %get-tuple-element.255, f32[1,2,128,128]{3,0,2,1:T(1,128)S(1)} %bitcast.173, s32[]{:T(128)S(6)} %copy.157, s32[]{:T(128)} %constant.159.clone.1..sunk.1, s32[]{:T(128)} %constant.159.clone.1..sunk.1, s32[]{:T(128)} %constant.159.clone.1..sunk.1) | dynamic-update-slice | bytes 262148 | tf_op jit(solution)/shard_map/vmap()/gather
  34.7 0.1 fusion.9
  34.8 0.1 copy.63
  34.9 0.6 fusion.50
  35.5 0.1 copy.64
  35.7 0.6 fusion.46
  36.2 0.6 fusion.3
  36.8 0.6 fusion.32
  37.5 0.6 fusion.48
  38.1 0.6 fusion.2
  38.7 0.6 convolution_add_fusion.1
  39.4 0.6 convolution_subtract_fusion.1
  40.0 0.7 fusion.39
  40.8 0.7 fusion.43
  41.5 0.8 fusion
  42.3 0.6 fusion.28
  42.9 0.6 fusion.37
  43.6 0.7 fusion.1
  44.4 0.6 fusion.41
  45.0 0.6 fusion.26
  45.7 0.6 fusion.11
  46.3 2.1 %convolution_bitcast_fusion = f32[2,16,128,128]{3,1,2,0:T(8,128)S(1)} fusion(f32[1,3,128,128]{3,1,2,0:T(4,128)S(1)} %get-tuple-element.179, f32[1,3,128,128]{3,1,2,0:T(4,128)S(1)} %get-tuple-element.178, f32[1,1,3,16]{3,1,2,0:T(1,128)S(1)} %copy-done.3), kind=kOutput, calls=%fused_computation.6 | convolution fusion | flops 18972672 | bytes 2490560 | tf_op jit(solution)/shard_map/sk,csij->ckij/dot_general | solution.py:108
  48.4 1.9 %copy.84 = f32[2,16,128,128]{3,2,1,0:T(8,128)} copy(f32[2,16,128,128]{3,1,2,0:T(8,128)S(1)} %convolution_bitcast_fusion) | data formatting | bytes 4194304 | tf_op jit(solution)/shard_map/sk,csij->ckij/transpose | solution.py:108
  50.6 0.2 pad_maximum_fusion
  50.8 0.3 copy-done.2
  51.1 21.9 %while.18 = (s32[]{:T(128)}, f32[3,256,256]{2,1,0:T(8,128)S(1)}, s32[3,2]{0,1:T(2,128)S(1)}, f32[3,3,128,128]{3,0,2,1:T(4,128)S(1)}, s32[]{:T(128)}, /*index=5*/s32[]{:T(128)}, s32[]{:T(128)}) while((s32[]{:T(128)}, f32[3,256,256]{2,1,0:T(8,128)S(1)}, s32[3,2]{0,1:T(2,128)S(1)}, f32[3,3,128,128]{3,0,2,1:T(4,128)S(1)}, s32[]{:T(128)}, ...), condition=%wide.region_1.2_spmd, body=%wide.region_0.0_spmd.sunk | while | flops 49160 | bytes 1376445 | solution.py:92
  51.1 0.2 constant_dynamic-slice_fusion.9
  51.3 0.6 constant_dynamic-slice_fusion.10
  55.5 0.1 dynamic-slice_add_fusion.2
  55.6 2.8 %dynamic_update_slice.8 = f32[3,256,256]{2,1,0:T(8,128)S(1)} dynamic-update-slice(f32[3,256,256]{2,1,0:T(8,128)S(1)} %get-tuple-element.272, f32[3,128,128]{2,1,0:T(8,128)S(1)} %dynamic-slice_add_fusion.2, s32[]{:T(128)} %constant.159.clone.1..sunk, s32[]{:T(128)S(6)} %select_n.170, s32[]{:T(128)S(6)} %select_n.171) | dynamic-update-slice | bytes 393220 | tf_op jit(solution)/shard_map/while/body/eval_jaxpr/dynamic_update_slice | solution.py:89
  58.4 0.2 constant_dynamic-slice_fusion.9
  58.6 0.6 constant_dynamic-slice_fusion.10
  62.9 2.7 %dynamic_update_slice.8 = f32[3,256,256]{2,1,0:T(8,128)S(1)} dynamic-update-slice(f32[3,256,256]{2,1,0:T(8,128)S(1)} %get-tuple-element.272, f32[3,128,128]{2,1,0:T(8,128)S(1)} %dynamic-slice_add_fusion.2, s32[]{:T(128)} %constant.159.clone.1..sunk, s32[]{:T(128)S(6)} %select_n.170, s32[]{:T(128)S(6)} %select_n.171) | dynamic-update-slice | bytes 393220 | tf_op jit(solution)/shard_map/while/body/eval_jaxpr/dynamic_update_slice | solution.py:89
  65.7 0.2 constant_dynamic-slice_fusion.9
  65.9 0.6 constant_dynamic-slice_fusion.10
  70.2 2.8 %dynamic_update_slice.8 = f32[3,256,256]{2,1,0:T(8,128)S(1)} dynamic-update-slice(f32[3,256,256]{2,1,0:T(8,128)S(1)} %get-tuple-element.272, f32[3,128,128]{2,1,0:T(8,128)S(1)} %dynamic-slice_add_fusion.2, s32[]{:T(128)} %constant.159.clone.1..sunk, s32[]{:T(128)S(6)} %select_n.170, s32[]{:T(128)S(6)} %select_n.171) | dynamic-update-slice | bytes 393220 | tf_op jit(solution)/shard_map/while/body/eval_jaxpr/dynamic_update_slice | solution.py:89
  73.1 2.3 %collective-permute-start.2 = (f32[3,256,128]{2,1,0:T(8,128)S(1)}, f32[3,256,128]{2,1,0:T(8,128)S(1)}, u32[]{:S(2)}, u32[]{:S(2)}) collective-permute-start(f32[3,256,128]{2,1,0:T(8,128)S(1)} %slice.92), channel_id=1, source_target_pairs={{0,1},{1,2},{2,3},{3,0},{4,5},{5,6},{6,7},{7,4},{8,9},{9,10},{10,1... | collective-permute-start | bytes 1179656 | tf_op jit(solution)/shard_map/ppermute | solution.py:13
  75.4 5.6 %collective-permute-done.2 = f32[3,256,128]{2,1,0:T(8,128)S(1)} collective-permute-done((f32[3,256,128]{2,1,0:T(8,128)S(1)}, f32[3,256,128]{2,1,0:T(8,128)S(1)}, u32[]{:S(2)}, u32[]{:S(2)}) %collective-permute-start.2) | collective-permute-done | bytes 393248 | tf_op jit(solution)/shard_map/ppermute | solution.py:13
  81.1 0.4 collective-permute-start.3
  81.5 12.8 %collective-permute-done.3 = f32[3,128,128]{2,1,0:T(8,128)S(1)} collective-permute-done((f32[3,128,128]{2,1,0:T(8,128)S(1)}, f32[3,128,128]{2,1,0:T(8,128)S(1)}, u32[]{:S(2)}, u32[]{:S(2)}) %collective-permute-start.3) | collective-permute-done | bytes 196640 | tf_op jit(solution)/shard_map/ppermute | solution.py:13
  94.3 0.6 slice_reduce_fusion
  94.9 6.3 %all-reduce = (f32[]{:T(128)}, f32[16]{0:T(128)S(1)}) all-reduce(f32[]{:T(128)} %slice_reduce_fusion, f32[16]{0:T(128)S(1)} %fusion.80), channel_id=1, replica_groups=mesh['grp'=2,'tx'=4,'ty'=4] {'ty'}, use_global_device_ids=true, to_apply=%region_3.4 | all-reduce | flops 17 | bytes 136 | tf_op jit(solution)/shard_map/psum | solution.py:101
  101.2 10.7 %all-reduce.1 = (f32[]{:T(128)}, f32[16]{0:T(128)S(1)}) all-reduce(f32[]{:T(128)} %get-tuple-element.170, f32[16]{0:T(128)S(1)} %get-tuple-element.171), channel_id=1, replica_groups=mesh['grp'=2,'tx'=4,'ty'=4] {'tx'}, use_global_device_ids=true, to_apply=%region_4.5 | all-reduce | flops 17 | bytes 136 | tf_op jit(solution)/shard_map/psum | solution.py:101
  112.0 3.3 %reduce-scatter.2.cloned.1.call-done = f32[256,128]{1,0:T(8,128)} async-done(((f32[4096,128]{1,0:T(8,128)}), f32[256,128]{1,0:T(8,128)}) %reduce-scatter.2.cloned.1.call-update) | async-done | bytes 131088 | tf_op jit(solution)/shard_map/reduce_scatter | solution.py:112
  115.3 1.7 convert_add_fusion
  117.6 0.7 fusion.22
  118.3 40.2 %all-gather.2.cloned.1.call-done = f32[4096,128]{1,0:T(8,128)} async-done(((f32[256,128]{1,0:T(8,128)}), f32[4096,128]{1,0:T(8,128)}) %all-gather.2.cloned.1.call-update) | async-done | bytes 2097168 | tf_op jit(solution)/shard_map/all_gather | solution.py:115
  158.5 3.1 %copy.169 = f32[2,16,128,128]{3,2,1,0:T(8,128)} copy(f32[2,16,128,128]{3,2,1,0:T(8,128)} %bitcast.175) | data formatting | bytes 4194304
  (34 shorter events, 1.0 us)
Async XLA Ops:
  7.2 108.1 %reduce-scatter.2.cloned.1.call-start = ((), (), s32[]{:S(2)}) async-start(), calls=%async_computation.1 | async-start | bytes 2228224 | tf_op jit(solution)/shard_map/reduce_scatter | solution.py:112
  7.2 8.2 %collective-permute-start = (f32[2,128,128]{2,1,0:T(8,128)}, f32[2,128,128]{2,1,0:T(8,128)S(1)}, u32[]{:S(2)}, u32[]{:S(2)}) collective-permute-start(f32[2,128,128]{2,1,0:T(8,128)} %param.16), channel_id=1, source_target_pairs={{0,12},{4,0},{8,4},{12,8},{1,13},{5,1},{9,5},{13,9},{2,14},{6,2},{... | collective-permute-start | bytes 393224 | tf_op jit(solution)/shard_map/ppermute | solution.py:13
  15.4 4.0 %collective-permute-start.1 = (f32[2,256,128]{2,1,0:T(8,128)S(1)}, f32[2,256,128]{2,1,0:T(8,128)S(1)}, u32[]{:S(2)}, u32[]{:S(2)}) collective-permute-start(f32[2,256,128]{2,1,0:T(8,128)S(1)} %constant_dynamic-update-slice_fusion), channel_id=1, source_target_pairs={{0,3},{1,0},{2,1},{3,2},{4,7},{5,4},{6,5},{7,6},{8,11},{9,8},{10,9... | collective-permute-start | bytes 786440 | tf_op jit(solution)/shard_map/ppermute | solution.py:13
  35.5 4.5 %copy-start.1 = (bf16[1,1,3,128,128]{4,3,2,1,0:T(8,128)(2,1)S(1)}, bf16[1,1,3,128,128]{4,3,2,1,0:T(8,128)(2,1)}, u32[]{:S(2)}) copy-start(bf16[1,1,3,128,128]{4,3,2,1,0:T(8,128)(2,1)} %param.21) | copy-start | bytes 294916
  43.6 2.7 %copy-start.3 = (f32[1,1,3,16]{3,1,2,0:T(1,128)S(1)}, f32[1,1,3,16]{3,1,2,0:T(1,128)}, u32[]{:S(2)}) copy-start(f32[1,1,3,16]{3,1,2,0:T(1,128)} %param.18) | copy-start | bytes 580
  50.4 0.7 copy-start.2
  50.4 108.1 %all-gather.2.cloned.1.call-start = ((), (), s32[]{:S(2)}) async-start(), calls=%async_computation.2 | async-start | bytes 2228224 | tf_op jit(solution)/shard_map/all_gather | solution.py:115
  73.0 44.6 %copy-start = (f32[2,128,128]{2,1,0:T(8,128)S(1)}, f32[2,128,128]{2,1,0:T(8,128)}, u32[]{:S(2)}) copy-start(f32[2,128,128]{2,1,0:T(8,128)} %param.16) | copy-start | bytes 393220
  73.1 7.9 %collective-permute-start.2 = (f32[3,256,128]{2,1,0:T(8,128)S(1)}, f32[3,256,128]{2,1,0:T(8,128)S(1)}, u32[]{:S(2)}, u32[]{:S(2)}) collective-permute-start(f32[3,256,128]{2,1,0:T(8,128)S(1)} %slice.92), channel_id=1, source_target_pairs={{0,1},{1,2},{2,3},{3,0},{4,5},{5,6},{6,7},{7,4},{8,9},{9,10},{10,1... | collective-permute-start | bytes 1179656 | tf_op jit(solution)/shard_map/ppermute | solution.py:13
  81.1 13.2 %collective-permute-start.3 = (f32[3,128,128]{2,1,0:T(8,128)S(1)}, f32[3,128,128]{2,1,0:T(8,128)S(1)}, u32[]{:S(2)}, u32[]{:S(2)}) collective-permute-start(f32[3,128,128]{2,1,0:T(8,128)S(1)} %slice.115), channel_id=1, source_target_pairs={{0,4},{4,8},{8,12},{12,0},{1,5},{5,9},{9,13},{13,1},{2,6},{6,10},{... | collective-permute-start | bytes 589832 | tf_op jit(solution)/shard_map/ppermute | solution.py:13
Sparse Core Ops, SparseCore 0:
  50.5 64.7 reduce-scatter.1
  118.0 40.4 all-gather.1
